TPU v7x, 256 devices: a whole 4x4x8 slice. The times are simulated.
256 devices in a mesh: px: 32 (over y, z_hi, core), py: 8 (over z_lo, x).
Axes of the slice: x: 4, y: 4, z: 8 (z_hi: 4, z_lo: 2; z = z_hi * 2 + z_lo), core: 2. Of those that a mesh axis runs over, the one named last changes fastest.
Arguments:
- charges_old: float32 [32, 8, 32, 32, 512], P('px', 'py'), may hold values from -0.0026758191 to 0.0026758191
- spline_moduli: float32 [3, 512], replicated, may hold values from 1 to 2.5
Outputs:
- structure: float32 [2, 512, 512, 512], P(None, 'px', 'py')
- energy: float32 [], replicated
- virial: float32 [6], replicated
All inputs are finite; a program needn't handle non-finite values.
Results may differ from a plain program's by a relative error of at most 0.0007.
Values sent between devices are 32-bit elements; how exact they have to be, the bound alone decides.
A program may use at most 128 MiB of HBM per device.

v0:
```python
import math

import jax
import jax.numpy as jnp
import numpy as np
from jax import lax
from jax.experimental import pallas as pl
from jax.experimental.pallas import tpu as pltpu
from jax.sharding import Mesh
from jax.sharding import PartitionSpec as P

AXES = ("px_0", "px_1", "px_2", "py_0", "py_1")
PX = AXES[:3]
PY = AXES[3:]
MESH = pl.DeviceIdType.MESH
F32 = jnp.float32
BF16 = jnp.bfloat16

beta_nm = 3.12
cell_nm = 0.1
N = 512
HALF = N // 2
NT = (((1,), (1,)), ((), ()))


def split_np(a):
    hi = a.astype(BF16)
    lo = (a - hi.astype(np.float64)).astype(BF16)
    return np.stack([hi, lo])


def angles(rows, cols):
    return 2.0 * math.pi * (np.outer(rows, cols) % N) / N


def z_table():
    z = np.arange(N)
    parts = []
    for b in range(4):
        t = angles(z, 64 * b + np.arange(64))
        parts += [np.cos(t), -np.sin(t)]
    edge = np.zeros((N, 128))
    for b in range(4):
        t = angles(z, np.array([64 * (b + 1)]))[:, 0]
        edge[:, 8 * b] = np.cos(t)
        edge[:, 64 + 8 * b] = -np.sin(t)
    return split_np(np.concatenate(parts + [edge], axis=1))


def half_table():
    r = np.arange(HALF)
    out = []
    for e in range(2):
        t = angles(2 * r + e, r)
        out.append(np.concatenate([np.cos(t), np.sin(t)], axis=1))
    return split_np(np.stack(out))


def split(v):
    hi = v.astype(BF16)
    return hi, (v - hi.astype(F32)).astype(BF16)


def mm(a, b):
    return jnp.dot(a, b, preferred_element_type=F32)


def signed_wave(mode_index):
    shifted = mode_index - N * (mode_index >= HALF).astype(jnp.int32)
    return shifted.astype(F32) / (cell_nm * N)


def ewald_kernel(
    mod_smem, mod_ref, x_hbm, wz_hbm, wh_hbm, out_hbm, energy_ref, virial_ref,
    x_ref, wz_ref, wh_ref, zs, r1, zy, r2, out_ref, acc, xz2, modxz, parts, first, middle, second,
    load, send1, recv1, send2, recv2, send3, recv3, leave,
):
    tables = ((x_hbm, x_ref), (wz_hbm, wz_ref), (wh_hbm, wh_ref))
    loads = [pltpu.make_async_copy(a, b, load.at[i]) for i, (a, b) in enumerate(tables)]
    for copy in loads:
        copy.start()

    yc, zh, c, lo, xc = [lax.axis_index(a) for a in AXES]
    p = yc * 8 + zh * 2 + c
    me16 = c * 8 + lo * 4 + xc
    me64 = p * 2 + lo
    outer = yc * 4 + zh
    b = xc + lo * (3 - 2 * xc)

    def peer16(t):
        d = lax.rem(me16 + t, 16)
        dc = lax.div(d, 8)
        dl = lax.rem(lax.div(d, 4), 2)
        dx = lax.rem(d, 4)
        return dc, dl, dx

    def peer64(t):
        d = lax.rem(me64 + t, 64)
        dp = lax.div(d, 2)
        dl = lax.rem(d, 2)
        dx = b + dl * (3 - 2 * b)
        return dp, dl, (lax.div(dp, 8), lax.rem(lax.div(dp, 2), 4), lax.rem(dp, 2), dl, dx)

    barrier = pltpu.get_barrier_semaphore()

    def greet16(t, carry):
        dc, dl, dx = peer16(t)
        pl.semaphore_signal(barrier, inc=1, device_id=(yc, zh, dc, dl, dx), device_id_type=MESH)
        return carry

    def greet64(t, carry):
        pl.semaphore_signal(barrier, inc=1, device_id=peer64(t)[2], device_id_type=MESH)
        return carry

    lax.fori_loop(1, 16, greet16, 0)
    lax.fori_loop(1, 64, greet64, 0)

    def z_step(g, carry):
        rows = x_ref[lax.div(g, 2), :, lax.rem(g, 2)].reshape(256, N)
        hi, low = split(rows)
        out = mm(hi, wz_ref[0]) + mm(low, wz_ref[0]) + mm(hi, wz_ref[1])
        for k in range(4):
            zs[g, k, 1:9] = out[:, 128 * k : 128 * k + 128].reshape(8, 32, 128)
        edge = out[:, 512:640].reshape(8, 32, 128)
        packed = edge[0]
        for r in range(1, 8):
            packed = packed + pltpu.roll(edge[r], r, 1)
        zs[g, 0, 0] = packed
        for k in range(1, 4):
            zs[g, k, 0] = pltpu.roll(packed, 128 - 8 * k, 1)
        return carry

    loads[0].wait()
    loads[1].wait()
    lax.fori_loop(0, 4, z_step, 0)
    pl.semaphore_wait(barrier, 78)

    my_rows = pl.ds(pl.multiple_of(me16 * 32, 32), 32)
    halves = (pl.ds(0, 5), pl.ds(5, 4))
    for h in range(2):

        def send_y(t, carry):
            dc, dl, dx = peer16(t)
            pltpu.make_async_remote_copy(
                src_ref=zs.at[2 * dc + dl, dx + dl * (3 - 2 * dx), halves[h]],
                dst_ref=r1.at[halves[h], my_rows, :],
                send_sem=send1.at[h],
                recv_sem=recv1.at[h],
                device_id=(yc, zh, dc, dl, dx),
                device_id_type=MESH,
            ).start()
            return carry

        lax.fori_loop(1, 16, send_y, 0)
    r1[:, my_rows, :] = zs[2 * c + lo, b]

    mx = signed_wave(lax.broadcasted_iota(jnp.int32, (1, N), 1))
    mz = signed_wave(64 * (4 * lo + xc) + lax.broadcasted_iota(jnp.int32, (64, 1), 0))
    acc[...] = jnp.zeros_like(acc)
    xz2[...] = mx * mx + mz * mz
    modz = pltpu.roll(jnp.broadcast_to(mod_ref[2:3, :], (8, N)), lax.rem(N - 64 * (4 * lo + xc), N), 1)
    modz = jnp.broadcast_to(modz[0:1, :128], (128, 128)).T[:64]
    modz = jnp.concatenate([modz] * 4, axis=1)
    modxz[...] = mod_ref[0:1, :] * modz * (1.0 / (math.pi * (cell_nm * N) ** 3))

    loads[2].wait()

    lane = lax.broadcasted_iota(jnp.int32, (HALF, 128), 1)
    is_edge = (lane == 0) | (lane == 64)
    turn = jnp.where(lane < 64, 1.0, -1.0).astype(F32)

    for h in range(2):
        many = r1.at[halves[h], pl.ds(0, 480), :]
        pltpu.make_async_copy(many, many, recv1.at[h]).wait()
        for e in range(2):
            base = MIRROR + 4 * (1 - e)

            def fold(i):
                top = r1[i, pl.ds(0, HALF), :]
                bottom = r1[i, pl.ds(HALF, HALF), :]
                return top + bottom if e == 0 else top - bottom

            for r in range(4):
                direct = fold(1 + 4 * h + r)
                edge = fold(0)
                if h or r:
                    edge = pltpu.roll(edge, 128 - (4 * h + r), 1)
                mirror = jnp.where(is_edge, edge, direct)
                plain = jnp.concatenate([direct, mirror], axis=1)
                turned = jnp.concatenate(
                    [pltpu.roll(direct, 64, 1) * turn, pltpu.roll(mirror, 64, 1) * turn], axis=1
                )
                hi, low = split(jnp.concatenate([plain, turned], axis=0))
                out = mm(wh_ref[0, e], hi) + mm(wh_ref[1, e], hi) + mm(wh_ref[0, e], low)
                zy[e, h, pl.ds(r, HALF, stride=4), :] = out[:, :128]
                zy[e, h, pl.ds(base + r, HALF, stride=4), :] = out[:, 128:]
                if e == 0:
                    zy[e, h, pl.ds(base + 4 * HALF + r, 1), :] = out[0:1, 128:]

            def rows_for(dp, dl):
                start = (1 - dl) * (32 * dp) + dl * (base + 4 * (249 - e) - 32 * dp)
                return zy.at[e, h, pl.ds(pl.multiple_of(start, 8), 32), :]

            own = (1 - lo) * (32 * p) + lo * (base + 4 * (249 - e) - 32 * p)
            r2[e, h, lo, p] = zy[e, h, pl.ds(pl.multiple_of(own, 8), 32), :]

            def send_x(t, carry):
                dp, dl, device = peer64(t)
                pltpu.make_async_remote_copy(
                    src_ref=rows_for(dp, dl),
                    dst_ref=r2.at[e, h, lo, p],
                    send_sem=send2.at[e, h],
                    recv_sem=recv2.at[e, h],
                    device_id=device,
                    device_id_type=MESH,
                ).start()
                return carry

            lax.fori_loop(1, 64, send_x, 0)

    flip = lo
    row = lax.broadcasted_iota(jnp.int32, (128, 128), 0)
    col = lax.broadcasted_iota(jnp.int32, (128, 128), 1)
    upper = row >= 64
    within = jnp.where(upper, row - 64, row)
    negated = jnp.where(within == 0, 0, 64 - within)
    target = jnp.where(flip == 1, negated, within) + jnp.where(upper, 64, 0)
    sign = jnp.where((flip == 1) & upper, -1.0, 1.0)
    select = jnp.where(col == target, sign, 0.0).astype(BF16)
    low_rows = lax.broadcasted_iota(jnp.int32, (32, 8, 128), 1) < 4

    def rows(v):
        return jnp.sum(v.reshape(8, 8, N), axis=0)

    for e in range(2):
        for h in range(2):
            many = zy.at[e, h, pl.ds(0, 63 * 32), :]
            pltpu.make_async_copy(many, many, recv2.at[e, h]).wait()

        def x_step(t, carry):
            tile = t + flip * (3 - 2 * t)

            def turned(a):
                top = r2[e, 0, a, :, pl.ds(pl.multiple_of(8 * tile, 8), 8), :]
                bottom = r2[e, 1, a, :, pl.ds(pl.multiple_of(8 * tile, 8), 8), :]
                slot0 = jnp.where(low_rows, top, pltpu.roll(bottom, 4, 1))
                slot1 = jnp.where(low_rows, pltpu.roll(top, 4, 1), bottom)
                his, lows = [], []
                for v in (jnp.where(flip == 1, slot1, slot0), jnp.where(flip == 1, slot0, slot1)):
                    hi, low = split(v.reshape(HALF, 128))
                    his.append(lax.dot_general(select, hi, NT, preferred_element_type=F32).astype(BF16))
                    lows.append(lax.dot_general(select, low, NT, preferred_element_type=F32).astype(BF16))
                hi, low = jnp.concatenate(his, axis=0), jnp.concatenate(lows, axis=0)
                return mm(hi, wh_ref[0, a]) + mm(low, wh_ref[0, a]) + mm(hi, wh_ref[1, a])

            even, odd = turned(0), turned(1)
            for j in range(2):

                def halves_of(v):
                    re, im = v[128 * j : 128 * j + 64], v[128 * j + 64 : 128 * j + 128]
                    return re[:, :HALF] + im[:, HALF:], im[:, :HALF] - re[:, HALF:]

                er, ei = halves_of(even)
                orr, oi = halves_of(odd)
                re = jnp.concatenate([er + orr, er - orr], axis=1)
                im = jnp.concatenate([ei + oi, ei - oi], axis=1)
                out_ref[0, 2 * t + j, e] = re
                out_ref[1, 2 * t + j, e] = im
                ky = 16 * p + 2 * (2 * t + j) + e
                my = (ky - jnp.where(ky >= HALF, N, 0)).astype(F32) * (1.0 / (cell_nm * N))
                mody = mod_smem[1, ky]
                msq = xz2[...] + my * my
                anchor = msq == 0.0
                inverse = 1.0 / jnp.where(anchor, 1.0, msq)
                decay = (math.pi**2 / beta_nm**2) * msq
                theta = jnp.where(anchor, 0.0, jnp.exp(-decay) * inverse * modxz[...] * mody)
                power = theta * (re * re + im * im)
                weight = power * (1.0 + decay) * inverse
                wz = weight * mz
                w0, w1, w2 = rows(weight), rows(wz), rows(wz * mz)
                acc[0] += rows(power)
                acc[1] += w0
                acc[2] += w0 * (my * my)
                acc[3] += w2
                acc[4] += w0 * my
                acc[5] += w1
                acc[6] += w1 * my
            block = pl.ds(2 * t, 2)
            pltpu.make_async_copy(out_ref.at[:, block, e], out_hbm.at[:, block, e], leave).start()
            return carry

        lax.fori_loop(0, 4, x_step, 0)

    def lanes(v):
        v = jnp.sum(v, axis=0, keepdims=True)
        return v[:, 0:128] + v[:, 128:256] + v[:, 256:384] + v[:, 384:512]

    parts[...] = jnp.concatenate(
        [
            lanes(acc[0]),
            lanes(acc[1] * (mx * mx)),
            lanes(acc[2]),
            lanes(acc[3]),
            lanes(acc[4] * mx),
            lanes(acc[5] * mx),
            lanes(acc[6]),
            jnp.zeros((1, 128), F32),
        ],
        axis=0,
    )

    def spread(stage, source, slots, me):
        slots[me] = source[...]

        def put(t, carry):
            if stage == 0:
                dc, dl, dx = peer16(t)
                device = (yc, zh, dc, dl, dx)
            else:
                d = lax.rem(outer + t, 16)
                device = (lax.div(d, 4), lax.rem(d, 4), c, lo, xc)
            pltpu.make_async_remote_copy(
                src_ref=source,
                dst_ref=slots.at[me],
                send_sem=send3.at[stage],
                recv_sem=recv3.at[stage],
                device_id=device,
                device_id_type=MESH,
            ).start()
            return carry

        lax.fori_loop(1, 16, put, 0)
        many = slots.at[pl.ds(0, 15)]
        pltpu.make_async_copy(many, many, recv3.at[stage]).wait()
        return jnp.sum(slots[...], axis=0)

    middle[...] = spread(0, parts, first, me16)
    totals = jnp.sum(spread(1, middle, second, outer), axis=1, keepdims=True)
    energy = 0.5 * totals[0:1]
    energy_ref[...] = jnp.broadcast_to(energy, (1, 128))
    sub8 = lax.broadcasted_iota(jnp.int32, (8, 128), 0)
    lane8 = lax.broadcasted_iota(jnp.int32, (8, 128), 1)
    full = jnp.where((sub8 >= 1) & (sub8 <= 3), energy, 0.0) - totals
    virial_ref[...] = jnp.sum(jnp.where(lane8 == sub8 - 1, full, 0.0), axis=0, keepdims=True)

    pltpu.make_async_copy(out_ref, out_hbm, leave).wait()
    for h in range(2):
        many = r1.at[halves[h], pl.ds(0, 480), :]
        pltpu.make_async_copy(many, many, send1.at[h]).wait()
        for e in range(2):
            sent = zy.at[e, h, pl.ds(0, 63 * 32), :]
            pltpu.make_async_copy(sent, sent, send2.at[e, h]).wait()
    for stage in range(2):
        many = first.at[pl.ds(0, 15)]
        pltpu.make_async_copy(many, many, send3.at[stage]).wait()


MIRROR = 1024
ROWS = 2064


def body(charges_old, spline_moduli):
    vmem, hbm = pl.BlockSpec(memory_space=pltpu.VMEM), pl.BlockSpec(memory_space=pl.ANY)
    dma = pltpu.SemaphoreType.DMA
    structure, energy, virial = pl.pallas_call(
        ewald_kernel,
        out_shape=(
            jax.ShapeDtypeStruct((2, 8, 2, 64, N), F32),
            jax.ShapeDtypeStruct((1, 128), F32),
            jax.ShapeDtypeStruct((1, 128), F32),
        ),
        in_specs=[pl.BlockSpec(memory_space=pltpu.SMEM), vmem] + [hbm] * 3,
        out_specs=(hbm, vmem, vmem),
        scratch_shapes=[
            pltpu.VMEM((2, 8, 2, 32, N), F32),
            pltpu.VMEM((2, N, 640), BF16),
            pltpu.VMEM((2, 2, HALF, N), BF16),
            pltpu.VMEM((4, 4, 9, 32, 128), F32),
            pltpu.VMEM((9, N, 128), F32),
            pltpu.VMEM((2, 2, ROWS, 128), F32),
            pltpu.VMEM((2, 2, 2, 32, 32, 128), F32),
            pltpu.VMEM((2, 8, 2, 64, N), F32),
            pltpu.VMEM((7, 8, N), F32),
            pltpu.VMEM((64, N), F32),
            pltpu.VMEM((64, N), F32),
            pltpu.VMEM((8, 128), F32),
            pltpu.VMEM((16, 8, 128), F32),
            pltpu.VMEM((8, 128), F32),
            pltpu.VMEM((16, 8, 128), F32),
            dma((3,)),
            dma((2,)),
            dma((2,)),
            dma((2, 2)),
            dma((2, 2)),
            dma((2,)),
            dma((2,)),
            dma,
        ],
        compiler_params=pltpu.CompilerParams(
            collective_id=0, has_side_effects=True, vmem_limit_bytes=62 * 2**20
        ),
        name="ewald",
    )(
        spline_moduli,
        spline_moduli,
        charges_old.reshape(2, 8, 2, 32, N),
        jnp.asarray(z_table()),
        jnp.asarray(half_table()),
    )
    return structure.reshape(2, 16, 64, N), energy[0, 0], virial[0, :6]


def solution(mesh):
    torus = Mesh(mesh.devices.reshape(4, 4, 2, 2, 4), AXES)
    return jax.shard_map(
        body,
        mesh=torus,
        in_specs=(P(PX, PY, None, None, None), P()),
        out_specs=(P(None, PX, PY, None), P(), P()),
        check_vma=False,
    )
```

profile of v0, /device:TPU:1, one launch (start us, length us, event | category | flops | bytes accessed | tf_op | source)
XLA Modules:
  0.0 155.7 jit_solution(16183326290354883171)
XLA Ops:
  0.6 147.8 %ewald.1 = (f32[2,8,2,64,512]{4,3,2,1,0:T(8,128)}, f32[1,128]{1,0:T(1,128)}, f32[1,128]{1,0:T(1,128)}) custom-call(f32[3,512]{1,0:T(4,128)} %mod_ref.1, f32[3,512]{1,0:T(4,128)} %mod_ref.1, f32[2,8,2,32,512]{4,3,2,1,0:T(8,128)} %bitcast.7, bf16[2,512,640]{2,1,0:T(8,128)(2,1)} %constant.4.clone.wz_hbm, bf16[2,2,256,512]{3,2,1,0:T(8,128)(2,1)} %constant.5.clone.wh_hbm), custom_call_target="tpu_custom_call" | custom-call | tf_op jit(solution)/shard_map/ewald/pallas_call | solution.py:365
  148.5 1.1 slice_bitcast_fusion
  149.6 0.0 copy-start
  149.6 4.9 %copy.9 = f32[2,16,64,512]{3,2,1,0:T(8,128)} copy(f32[2,16,64,512]{3,2,1,0:T(8,128)} %bitcast.6) | data formatting | bytes 8388608
  154.5 0.0 copy-done
Async XLA Ops:
  149.6 4.9 %copy-start = (f32[1,128]{1,0:T(1,128)S(1)}, f32[1,128]{1,0:T(1,128)}, u32[]{:S(2)}) copy-start(f32[1,128]{1,0:T(1,128)} %get-tuple-element.7) | copy-start | bytes 1540
where the time goes:
time: 156 us
  Pallas kernels  148 us (95%)
  local copies, waits for them, and re-layouts  6.02 us (4%)
  between operations  1.81 us (1%)
    pallas_call x1, Pallas kernels, body(): pl.pallas_call(ewald_kernel, out_shape=(jax.ShapeDtypeStruct((2, 8, 2, 64...  148 us
    unnamed x3, local copies, waits for them, and re-layouts  4.92 us

commit v1 on v0

--- a/solution.py
+++ b/solution.py
@@ -109,25 +109,34 @@
         return carry
 
     def greet64(t, carry):
-        pl.semaphore_signal(barrier, inc=1, device_id=peer64(t)[2], device_id_type=MESH)
+        far = lax.rem(t + 24, 63) + 1
+        pl.semaphore_signal(barrier, inc=1, device_id=peer64(far)[2], device_id_type=MESH)
         return carry
 
+    lax.fori_loop(0, 63, greet64, 0)
     lax.fori_loop(1, 16, greet16, 0)
-    lax.fori_loop(1, 64, greet64, 0)
+
+    narrow = lax.rem(lax.broadcasted_iota(jnp.int32, (32, 128), 1), 64) < 8
 
     def z_step(g, carry):
         rows = x_ref[lax.div(g, 2), :, lax.rem(g, 2)].reshape(256, N)
         hi, low = split(rows)
         out = mm(hi, wz_ref[0]) + mm(low, wz_ref[0]) + mm(hi, wz_ref[1])
         for k in range(4):
-            zs[g, k, 1:9] = out[:, 128 * k : 128 * k + 128].reshape(8, 32, 128)
+            zs[g, k, 8:264] = out[:, 128 * k : 128 * k + 128]
         edge = out[:, 512:640].reshape(8, 32, 128)
         packed = edge[0]
         for r in range(1, 8):
             packed = packed + pltpu.roll(edge[r], r, 1)
-        zs[g, 0, 0] = packed
-        for k in range(1, 4):
-            zs[g, k, 0] = pltpu.roll(packed, 128 - 8 * k, 1)
+        for k in range(4):
+            one = pltpu.roll(packed, 128 - 8 * k, 1) if k else packed
+            one = jnp.where(narrow, one, 0.0).reshape(4, 8, 128)
+            zs[g, k, 0:8] = (
+                one[0]
+                + pltpu.roll(one[1], 8, 1)
+                + pltpu.roll(one[2], 16, 1)
+                + pltpu.roll(one[3], 24, 1)
+            )
         return carry
 
     loads[0].wait()
@@ -135,15 +144,14 @@
     lax.fori_loop(0, 4, z_step, 0)
     pl.semaphore_wait(barrier, 78)
 
-    my_rows = pl.ds(pl.multiple_of(me16 * 32, 32), 32)
-    halves = (pl.ds(0, 5), pl.ds(5, 4))
+    halves = (pl.ds(0, 136), pl.ds(136, 128))
     for h in range(2):
 
         def send_y(t, carry):
             dc, dl, dx = peer16(t)
             pltpu.make_async_remote_copy(
                 src_ref=zs.at[2 * dc + dl, dx + dl * (3 - 2 * dx), halves[h]],
-                dst_ref=r1.at[halves[h], my_rows, :],
+                dst_ref=r1.at[me16, halves[h]],
                 send_sem=send1.at[h],
                 recv_sem=recv1.at[h],
                 device_id=(yc, zh, dc, dl, dx),
@@ -152,7 +160,7 @@
             return carry
 
         lax.fori_loop(1, 16, send_y, 0)
-    r1[:, my_rows, :] = zs[2 * c + lo, b]
+    r1[me16] = zs[2 * c + lo, b]
 
     mx = signed_wave(lax.broadcasted_iota(jnp.int32, (1, N), 1))
     mz = signed_wave(64 * (4 * lo + xc) + lax.broadcasted_iota(jnp.int32, (64, 1), 0))
@@ -170,21 +178,24 @@
     turn = jnp.where(lane < 64, 1.0, -1.0).astype(F32)
 
     for h in range(2):
-        many = r1.at[halves[h], pl.ds(0, 480), :]
+        many = r1.at[pl.ds(0, 15), halves[h]]
         pltpu.make_async_copy(many, many, recv1.at[h]).wait()
         for e in range(2):
             base = MIRROR + 4 * (1 - e)
 
-            def fold(i):
-                top = r1[i, pl.ds(0, HALF), :]
-                bottom = r1[i, pl.ds(HALF, HALF), :]
+            def fold(first, count):
+                top = r1[0:8, first : first + count]
+                bottom = r1[8:16, first : first + count]
                 return top + bottom if e == 0 else top - bottom
 
+            edges = fold(0, 8)
             for r in range(4):
-                direct = fold(1 + 4 * h + r)
-                edge = fold(0)
-                if h or r:
-                    edge = pltpu.roll(edge, 128 - (4 * h + r), 1)
+                i = 4 * h + r
+                direct = fold(8 + 32 * i, 32).reshape(HALF, 128)
+                edge = jnp.stack(
+                    [pltpu.roll(edges, 128 - 8 * k - i, 2) if k + i else edges for k in range(4)],
+                    axis=1,
+                ).reshape(HALF, 128)
                 mirror = jnp.where(is_edge, edge, direct)
                 plain = jnp.concatenate([direct, mirror], axis=1)
                 turned = jnp.concatenate(
@@ -197,26 +208,29 @@
                 if e == 0:
                     zy[e, h, pl.ds(base + 4 * HALF + r, 1), :] = out[0:1, 128:]
 
-            def rows_for(dp, dl):
-                start = (1 - dl) * (32 * dp) + dl * (base + 4 * (249 - e) - 32 * dp)
-                return zy.at[e, h, pl.ds(pl.multiple_of(start, 8), 32), :]
-
-            own = (1 - lo) * (32 * p) + lo * (base + 4 * (249 - e) - 32 * p)
-            r2[e, h, lo, p] = zy[e, h, pl.ds(pl.multiple_of(own, 8), 32), :]
-
-            def send_x(t, carry):
-                dp, dl, device = peer64(t)
-                pltpu.make_async_remote_copy(
-                    src_ref=rows_for(dp, dl),
-                    dst_ref=r2.at[e, h, lo, p],
-                    send_sem=send2.at[e, h],
-                    recv_sem=recv2.at[e, h],
-                    device_id=device,
-                    device_id_type=MESH,
-                ).start()
-                return carry
-
-            lax.fori_loop(1, 64, send_x, 0)
+            def start_for(dp, dl):
+                return (1 - dl) * (32 * dp) + dl * (base + 4 * (249 - e) - 32 * dp)
+
+            r2[e, h, lo, p] = zy[e, h, pl.ds(pl.multiple_of(start_for(p, lo), 8), 32), :]
+            pieces = 2 if e and h else 1
+            size = 32 // pieces
+            for piece in range(pieces):
+
+                def send_x(t, carry):
+                    dp, dl, device = peer64(t)
+                    skip = size * (piece + dl * (pieces - 1 - 2 * piece))
+                    start = start_for(dp, dl) + skip
+                    pltpu.make_async_remote_copy(
+                        src_ref=zy.at[e, h, pl.ds(pl.multiple_of(start, 8), size), :],
+                        dst_ref=r2.at[e, h, lo, p, pl.ds(pl.multiple_of(skip, 8), size), :],
+                        send_sem=send2.at[2 * h + e + piece],
+                        recv_sem=recv2.at[2 * h + e + piece],
+                        device_id=device,
+                        device_id_type=MESH,
+                    ).start()
+                    return carry
+
+                lax.fori_loop(1, 64, send_x, 0)
 
     flip = lo
     row = lax.broadcasted_iota(jnp.int32, (128, 128), 0)
@@ -233,9 +247,14 @@
         return jnp.sum(v.reshape(8, 8, N), axis=0)
 
     for e in range(2):
-        for h in range(2):
-            many = zy.at[e, h, pl.ds(0, 63 * 32), :]
-            pltpu.make_async_copy(many, many, recv2.at[e, h]).wait()
+
+        def arrived(block, size):
+            many = zy.at[0, 0, pl.ds(0, 63 * size), :]
+            pltpu.make_async_copy(many, many, recv2.at[block]).wait()
+
+        arrived(e, 32)
+        if e == 0:
+            arrived(2, 32)
 
         def x_step(t, carry):
             tile = t + flip * (3 - 2 * t)
@@ -289,7 +308,13 @@
             pltpu.make_async_copy(out_ref.at[:, block, e], out_hbm.at[:, block, e], leave).start()
             return carry
 
-        lax.fori_loop(0, 4, x_step, 0)
+        if e == 0:
+            lax.fori_loop(0, 4, x_step, 0)
+        else:
+            for piece in range(2):
+                arrived(3 + piece, 16)
+                x_step(2 * piece, 0)
+                x_step(2 * piece + 1, 0)
 
     def lanes(v):
         v = jnp.sum(v, axis=0, keepdims=True)
@@ -337,24 +362,57 @@
     middle[...] = spread(0, parts, first, me16)
     totals = jnp.sum(spread(1, middle, second, outer), axis=1, keepdims=True)
     energy = 0.5 * totals[0:1]
-    energy_ref[...] = jnp.broadcast_to(energy, (1, 128))
+    energy_ref[...] = energy
     sub8 = lax.broadcasted_iota(jnp.int32, (8, 128), 0)
     lane8 = lax.broadcasted_iota(jnp.int32, (8, 128), 1)
     full = jnp.where((sub8 >= 1) & (sub8 <= 3), energy, 0.0) - totals
-    virial_ref[...] = jnp.sum(jnp.where(lane8 == sub8 - 1, full, 0.0), axis=0, keepdims=True)
+    virial_ref[...] = jnp.sum(jnp.where(lane8 == sub8 - 1, full, 0.0), axis=0, keepdims=True)[:, :6]
 
     pltpu.make_async_copy(out_ref, out_hbm, leave).wait()
     for h in range(2):
-        many = r1.at[halves[h], pl.ds(0, 480), :]
+        many = r1.at[pl.ds(0, 15), halves[h]]
         pltpu.make_async_copy(many, many, send1.at[h]).wait()
-        for e in range(2):
-            sent = zy.at[e, h, pl.ds(0, 63 * 32), :]
-            pltpu.make_async_copy(sent, sent, send2.at[e, h]).wait()
+    for block, size in enumerate((32, 32, 32, 16, 16)):
+        sent = zy.at[0, 0, pl.ds(0, 63 * size), :]
+        pltpu.make_async_copy(sent, sent, send2.at[block]).wait()
     for stage in range(2):
         many = first.at[pl.ds(0, 15)]
         pltpu.make_async_copy(many, many, send3.at[stage]).wait()
 
 
+def copy_kernel(source, target, buffer, read, write):
+    reads = [
+        pltpu.make_async_copy(source.at[i], buffer.at[i], read.at[i]) for i in range(PIECES)
+    ]
+    writes = [
+        pltpu.make_async_copy(buffer.at[i], target.at[i], write.at[i]) for i in range(PIECES)
+    ]
+    for copy in reads:
+        copy.start()
+    for i in range(PIECES):
+        reads[i].wait()
+        writes[i].start()
+    for copy in writes:
+        copy.wait()
+
+
+def copy_out(array):
+    return pl.pallas_call(
+        copy_kernel,
+        out_shape=jax.ShapeDtypeStruct(array.shape, F32),
+        in_specs=[pl.BlockSpec(memory_space=pl.ANY)],
+        out_specs=pl.BlockSpec(memory_space=pl.ANY),
+        scratch_shapes=[
+            pltpu.VMEM(array.shape, F32),
+            pltpu.SemaphoreType.DMA((PIECES,)),
+            pltpu.SemaphoreType.DMA((PIECES,)),
+        ],
+        compiler_params=pltpu.CompilerParams(vmem_limit_bytes=62 * 2**20),
+        name="copy_out",
+    )(array)
+
+
+PIECES = 16
 MIRROR = 1024
 ROWS = 2064
 
@@ -366,8 +424,8 @@
         ewald_kernel,
         out_shape=(
             jax.ShapeDtypeStruct((2, 8, 2, 64, N), F32),
-            jax.ShapeDtypeStruct((1, 128), F32),
-            jax.ShapeDtypeStruct((1, 128), F32),
+            jax.ShapeDtypeStruct((1, 1), F32),
+            jax.ShapeDtypeStruct((1, 6), F32),
         ),
         in_specs=[pl.BlockSpec(memory_space=pltpu.SMEM), vmem] + [hbm] * 3,
         out_specs=(hbm, vmem, vmem),
@@ -375,8 +433,8 @@
             pltpu.VMEM((2, 8, 2, 32, N), F32),
             pltpu.VMEM((2, N, 640), BF16),
             pltpu.VMEM((2, 2, HALF, N), BF16),
-            pltpu.VMEM((4, 4, 9, 32, 128), F32),
-            pltpu.VMEM((9, N, 128), F32),
+            pltpu.VMEM((4, 4, 264, 128), F32),
+            pltpu.VMEM((16, 264, 128), F32),
             pltpu.VMEM((2, 2, ROWS, 128), F32),
             pltpu.VMEM((2, 2, 2, 32, 32, 128), F32),
             pltpu.VMEM((2, 8, 2, 64, N), F32),
@@ -390,8 +448,8 @@
             dma((3,)),
             dma((2,)),
             dma((2,)),
-            dma((2, 2)),
-            dma((2, 2)),
+            dma((5,)),
+            dma((5,)),
             dma((2,)),
             dma((2,)),
             dma,
@@ -407,7 +465,8 @@
         jnp.asarray(z_table()),
         jnp.asarray(half_table()),
     )
-    return structure.reshape(2, 16, 64, N), energy[0, 0], virial[0, :6]
+    structure = copy_out(structure.reshape(PIECES, -1, N))
+    return structure.reshape(2, 16, 64, N), energy[0, 0], virial[0]
 
 
 def solution(mesh):

time: 156 us -> 151 us (0.968)
  local copies, waits for them, and re-layouts: 6.02 us -> 0.52 us
    unnamed x3, local copies, waits for them, and re-layouts: 4.92 us -> 0.52 us
    pallas_call x0 -> x1, Pallas kernels: none -> 3.85 us  [copy_out(): pl.pallas_call(copy_kernel, out_shape=jax.ShapeDtypeStruct(array.shape, F...]
    pallas_call x1, Pallas kernels: 148 us -> 144 us  [body(): pl.pallas_call(ewald_kernel, out_shape=(jax.ShapeDtypeStruct((2, 8, 2, 64...]
where the time goes in v1:
time: 151 us
  Pallas kernels  148 us (98%)
  between operations  2.48 us (2%)
    pallas_call x1, Pallas kernels, body(): pl.pallas_call(ewald_kernel, out_shape=(jax.ShapeDtypeStruct((2, 8, 2, 64...  144 us
    pallas_call x1, Pallas kernels, copy_out(): pl.pallas_call(copy_kernel, out_shape=jax.ShapeDtypeStruct(array.shape, F...  3.85 us

profile of v1, /device:TPU:1, one launch (start us, length us, event | category | flops | bytes accessed | tf_op | source)
XLA Modules:
  0.0 150.9 jit_solution(10446013256890005037)
XLA Ops:
  0.6 144.0 %ewald.1 = (f32[2,8,2,64,512]{4,3,2,1,0:T(8,128)}, f32[1,1]{1,0:T(1,128)}, f32[1,6]{1,0:T(1,128)}) custom-call(f32[3,512]{1,0:T(4,128)} %mod_ref.1, f32[3,512]{1,0:T(4,128)} %mod_ref.1, f32[2,8,2,32,512]{4,3,2,1,0:T(8,128)} %bitcast.7, bf16[2,512,640]{2,1,0:T(8,128)(2,1)} %constant.4.clone.wz_hbm, bf16[2,2,256,512]{3,2,1,0:T(8,128)(2,1)} %constant.5.clone.wh_hbm), custom_call_target="tpu_custom_call" | custom-call | tf_op jit(solution)/shard_map/ewald/pallas_call | solution.py:423
  144.6 0.0 copy-start
  144.6 3.9 %copy_out.1 = f32[16,128,512]{2,1,0:T(8,128)} custom-call(f32[16,128,512]{2,1,0:T(8,128)} %bitcast.6), custom_call_target="tpu_custom_call" | custom-call | tf_op jit(solution)/shard_map/copy_out/pallas_call | solution.py:400
  149.2 0.0 copy-done
  149.2 0.5 copy.10
Async XLA Ops:
  144.6 4.6 %copy-start = (f32[1,6]{1,0:T(1,128)S(1)}, f32[1,6]{1,0:T(1,128)}, u32[]{:S(2)}) copy-start(f32[1,6]{1,0:T(1,128)} %get-tuple-element.8) | copy-start | bytes 76

commit v2 on v1

--- a/solution.py
+++ b/solution.py
@@ -71,11 +71,13 @@
 
 
 def ewald_kernel(
-    mod_smem, mod_ref, x_hbm, wz_hbm, wh_hbm, out_hbm, energy_ref, virial_ref,
-    x_ref, wz_ref, wh_ref, zs, r1, zy, r2, out_ref, acc, xz2, modxz, parts, first, middle, second,
-    load, send1, recv1, send2, recv2, send3, recv3, leave,
+    mod_hbm, x_hbm, wz_hbm, wh_hbm, out_ref, energy_ref, virial_ref,
+    mod_smem, mod_ref, x_ref, wz_ref, wh_ref, zs, r1, zy, r2, acc, xz2, modxz, parts, first, middle, second,
+    load, send1, recv1, send2, recv2, send3, recv3,
 ):
-    tables = ((x_hbm, x_ref), (wz_hbm, wz_ref), (wh_hbm, wh_ref))
+    tables = (
+        (x_hbm, x_ref), (wz_hbm, wz_ref), (wh_hbm, wh_ref), (mod_hbm, mod_ref), (mod_hbm, mod_smem)
+    )
     loads = [pltpu.make_async_copy(a, b, load.at[i]) for i, (a, b) in enumerate(tables)]
     for copy in loads:
         copy.start()
@@ -113,8 +115,8 @@
         pl.semaphore_signal(barrier, inc=1, device_id=peer64(far)[2], device_id_type=MESH)
         return carry
 
-    lax.fori_loop(0, 63, greet64, 0)
-    lax.fori_loop(1, 16, greet16, 0)
+    lax.fori_loop(0, 63, greet64, 0, unroll=7)
+    lax.fori_loop(1, 16, greet16, 0, unroll=5)
 
     narrow = lax.rem(lax.broadcasted_iota(jnp.int32, (32, 128), 1), 64) < 8
 
@@ -148,7 +150,10 @@
     for h in range(2):
 
         def send_y(t, carry):
-            dc, dl, dx = peer16(t)
+            d = lax.rem(c * 4 + xc + t, 8)
+            dc, dx = lax.div(d, 4), lax.rem(d, 4)
+            stay = lax.div(t, 8)
+            dl = lo * stay + (1 - lo) * (1 - stay)
             pltpu.make_async_remote_copy(
                 src_ref=zs.at[2 * dc + dl, dx + dl * (3 - 2 * dx), halves[h]],
                 dst_ref=r1.at[me16, halves[h]],
@@ -159,9 +164,12 @@
             ).start()
             return carry
 
-        lax.fori_loop(1, 16, send_y, 0)
+        lax.fori_loop(0, 8, send_y, 0, unroll=8)
+        lax.fori_loop(9, 16, send_y, 0, unroll=7)
     r1[me16] = zs[2 * c + lo, b]
 
+    loads[3].wait()
+    loads[4].wait()
     mx = signed_wave(lax.broadcasted_iota(jnp.int32, (1, N), 1))
     mz = signed_wave(64 * (4 * lo + xc) + lax.broadcasted_iota(jnp.int32, (64, 1), 0))
     acc[...] = jnp.zeros_like(acc)
@@ -216,8 +224,14 @@
             size = 32 // pieces
             for piece in range(pieces):
 
-                def send_x(t, carry):
-                    dp, dl, device = peer64(t)
+                def send_x(k, turn_y):
+                    part = lax.div(k + 1, 2)
+                    dz = lax.rem(2 * zh + lo + 4 + part * (1 - 2 * lax.rem(k, 2)), 8)
+                    dzh, dl = lax.div(dz, 2), lax.rem(dz, 2)
+                    dy = lax.rem(yc + turn_y // 2, 4)
+                    dc = lax.rem(c + turn_y % 2, 2)
+                    dp = dy * 8 + dzh * 2 + dc
+                    device = (dy, dzh, dc, dl, b + dl * (3 - 2 * b))
                     skip = size * (piece + dl * (pieces - 1 - 2 * piece))
                     start = start_for(dp, dl) + skip
                     pltpu.make_async_remote_copy(
@@ -228,9 +242,15 @@
                         device_id=device,
                         device_id_type=MESH,
                     ).start()
+
+                def send_plane(k, carry):
+                    for i in range(8):
+                        send_x(k, i)
                     return carry
 
-                lax.fori_loop(1, 64, send_x, 0)
+                lax.fori_loop(0, 7, send_plane, 0)
+                for i in range(1, 8):
+                    send_x(7, i)
 
     flip = lo
     row = lax.broadcasted_iota(jnp.int32, (128, 128), 0)
@@ -304,8 +324,6 @@
                 acc[4] += w0 * my
                 acc[5] += w1
                 acc[6] += w1 * my
-            block = pl.ds(2 * t, 2)
-            pltpu.make_async_copy(out_ref.at[:, block, e], out_hbm.at[:, block, e], leave).start()
             return carry
 
         if e == 0:
@@ -354,7 +372,7 @@
             ).start()
             return carry
 
-        lax.fori_loop(1, 16, put, 0)
+        lax.fori_loop(1, 16, put, 0, unroll=5)
         many = slots.at[pl.ds(0, 15)]
         pltpu.make_async_copy(many, many, recv3.at[stage]).wait()
         return jnp.sum(slots[...], axis=0)
@@ -368,7 +386,6 @@
     full = jnp.where((sub8 >= 1) & (sub8 <= 3), energy, 0.0) - totals
     virial_ref[...] = jnp.sum(jnp.where(lane8 == sub8 - 1, full, 0.0), axis=0, keepdims=True)[:, :6]
 
-    pltpu.make_async_copy(out_ref, out_hbm, leave).wait()
     for h in range(2):
         many = r1.at[pl.ds(0, 15), halves[h]]
         pltpu.make_async_copy(many, many, send1.at[h]).wait()
@@ -380,39 +397,6 @@
         pltpu.make_async_copy(many, many, send3.at[stage]).wait()
 
 
-def copy_kernel(source, target, buffer, read, write):
-    reads = [
-        pltpu.make_async_copy(source.at[i], buffer.at[i], read.at[i]) for i in range(PIECES)
-    ]
-    writes = [
-        pltpu.make_async_copy(buffer.at[i], target.at[i], write.at[i]) for i in range(PIECES)
-    ]
-    for copy in reads:
-        copy.start()
-    for i in range(PIECES):
-        reads[i].wait()
-        writes[i].start()
-    for copy in writes:
-        copy.wait()
-
-
-def copy_out(array):
-    return pl.pallas_call(
-        copy_kernel,
-        out_shape=jax.ShapeDtypeStruct(array.shape, F32),
-        in_specs=[pl.BlockSpec(memory_space=pl.ANY)],
-        out_specs=pl.BlockSpec(memory_space=pl.ANY),
-        scratch_shapes=[
-            pltpu.VMEM(array.shape, F32),
-            pltpu.SemaphoreType.DMA((PIECES,)),
-            pltpu.SemaphoreType.DMA((PIECES,)),
-        ],
-        compiler_params=pltpu.CompilerParams(vmem_limit_bytes=62 * 2**20),
-        name="copy_out",
-    )(array)
-
-
-PIECES = 16
 MIRROR = 1024
 ROWS = 2064
 
@@ -427,9 +411,11 @@
             jax.ShapeDtypeStruct((1, 1), F32),
             jax.ShapeDtypeStruct((1, 6), F32),
         ),
-        in_specs=[pl.BlockSpec(memory_space=pltpu.SMEM), vmem] + [hbm] * 3,
-        out_specs=(hbm, vmem, vmem),
+        in_specs=[hbm] * 4,
+        out_specs=(vmem, vmem, vmem),
         scratch_shapes=[
+            pltpu.SMEM((3, N), F32),
+            pltpu.VMEM((3, N), F32),
             pltpu.VMEM((2, 8, 2, 32, N), F32),
             pltpu.VMEM((2, N, 640), BF16),
             pltpu.VMEM((2, 2, HALF, N), BF16),
@@ -437,7 +423,6 @@
             pltpu.VMEM((16, 264, 128), F32),
             pltpu.VMEM((2, 2, ROWS, 128), F32),
             pltpu.VMEM((2, 2, 2, 32, 32, 128), F32),
-            pltpu.VMEM((2, 8, 2, 64, N), F32),
             pltpu.VMEM((7, 8, N), F32),
             pltpu.VMEM((64, N), F32),
             pltpu.VMEM((64, N), F32),
@@ -445,27 +430,29 @@
             pltpu.VMEM((16, 8, 128), F32),
             pltpu.VMEM((8, 128), F32),
             pltpu.VMEM((16, 8, 128), F32),
-            dma((3,)),
+            dma((5,)),
             dma((2,)),
             dma((2,)),
             dma((5,)),
             dma((5,)),
             dma((2,)),
             dma((2,)),
-            dma,
         ],
         compiler_params=pltpu.CompilerParams(
-            collective_id=0, has_side_effects=True, vmem_limit_bytes=62 * 2**20
+            collective_id=0, has_side_effects=True, vmem_limit_bytes=24 * 2**20
         ),
         name="ewald",
     )(
-        spline_moduli,
-        spline_moduli,
-        charges_old.reshape(2, 8, 2, 32, N),
-        jnp.asarray(z_table()),
-        jnp.asarray(half_table()),
+        *[
+            pltpu.with_memory_space_constraint(operand, pltpu.HBM)
+            for operand in (
+                spline_moduli,
+                charges_old.reshape(2, 8, 2, 32, N),
+                jnp.asarray(z_table()),
+                jnp.asarray(half_table()),
+            )
+        ]
     )
-    structure = copy_out(structure.reshape(PIECES, -1, N))
     return structure.reshape(2, 16, 64, N), energy[0, 0], virial[0]
 
 

time: 151 us -> 147 us (0.974)
  Pallas kernels: 148 us -> 142 us
  local copies, waits for them, and re-layouts: 0.52 us -> 2.53 us
    pallas_call x1 -> x0, Pallas kernels: 3.85 us -> none  [copy_out(): pl.pallas_call(copy_kernel, out_shape=jax.ShapeDtypeStruct(array.shape, F...]
    pallas_call x1, Pallas kernels: 144 us -> 142 us  [body(): pl.pallas_call(ewald_kernel, out_shape=(jax.ShapeDtypeStruct((2, 8, 2, 64...]
    unnamed x3 -> x2, local copies, waits for them, and re-layouts: 0.52 us -> 2.53 us
where the time goes in v2:
time: 147 us
  Pallas kernels  142 us (97%)
  local copies, waits for them, and re-layouts  2.53 us (2%)
  between operations  2.33 us (2%)
    pallas_call x1, Pallas kernels, body(): pl.pallas_call(ewald_kernel, out_shape=(jax.ShapeDtypeStruct((2, 8, 2, 64...  142 us

profile of v2, /device:TPU:1, one launch (start us, length us, event | category | flops | bytes accessed | tf_op | source)
XLA Modules:
  0.0 146.7 jit_solution(6522623370497978234)
XLA Ops:
  0.6 141.8 %ewald.1 = (f32[2,8,2,64,512]{4,3,2,1,0:T(8,128)S(1)}, f32[1,1]{1,0:T(1,128)}, f32[1,6]{1,0:T(1,128)S(1)}) custom-call(f32[3,512]{1,0:T(4,128)} %mod_hbm.1, f32[2,8,2,32,512]{4,3,2,1,0:T(8,128)} %bitcast.6, bf16[2,512,640]{2,1,0:T(8,128)(2,1)} %constant.4.clone.wz_hbm, bf16[2,2,256,512]{3,2,1,0:T(8,128)(2,1)} %constant.5.clone.wh_hbm), custom_call_target="tpu_custom_call" | custom-call | tf_op jit(solution)/shard_map/ewald/pallas_call | solution.py:407
  142.5 2.0 %copy.10 = f32[2,16,64,512]{3,2,1,0:T(8,128)} copy(f32[2,16,64,512]{3,2,1,0:T(8,128)S(1)} %bitcast.4) | data formatting | bytes 8388608
  145.1 0.5 copy.12

commit v3 on v2

--- a/solution.py
+++ b/solution.py
@@ -72,7 +72,7 @@
 
 def ewald_kernel(
     mod_hbm, x_hbm, wz_hbm, wh_hbm, out_ref, energy_ref, virial_ref,
-    mod_smem, mod_ref, x_ref, wz_ref, wh_ref, zs, r1, zy, r2, acc, xz2, modxz, parts, first, middle, second,
+    mod_smem, mod_ref, x_ref, wz_ref, wh_ref, wy_ref, zs, r1, zy, r2, acc, xz2, modxz, parts, first, middle, second,
     load, send1, recv1, send2, recv2, send3, recv3,
 ):
     tables = (
@@ -146,7 +146,6 @@
     lax.fori_loop(0, 4, z_step, 0)
     pl.semaphore_wait(barrier, 78)
 
-    halves = (pl.ds(0, 136), pl.ds(136, 128))
     for h in range(2):
 
         def send_y(t, carry):
@@ -155,8 +154,8 @@
             stay = lax.div(t, 8)
             dl = lo * stay + (1 - lo) * (1 - stay)
             pltpu.make_async_remote_copy(
-                src_ref=zs.at[2 * dc + dl, dx + dl * (3 - 2 * dx), halves[h]],
-                dst_ref=r1.at[me16, halves[h]],
+                src_ref=zs.at[2 * dc + h, dx + dl * (3 - 2 * dx)],
+                dst_ref=r1.at[h, me16],
                 send_sem=send1.at[h],
                 recv_sem=recv1.at[h],
                 device_id=(yc, zh, dc, dl, dx),
@@ -166,7 +165,8 @@
 
         lax.fori_loop(0, 8, send_y, 0, unroll=8)
         lax.fori_loop(9, 16, send_y, 0, unroll=7)
-    r1[me16] = zs[2 * c + lo, b]
+    for h in range(2):
+        r1[h, me16] = zs[2 * c + h, b]
 
     loads[3].wait()
     loads[4].wait()
@@ -181,76 +181,87 @@
 
     loads[2].wait()
 
+    def plane(d):
+        dz = lax.rem(2 * zh + lo + 8 + d * (2 * lo - 1), 8)
+        return lax.div(dz, 2), lax.rem(dz, 2)
+
+    for kind in range(2):
+        for near in range(2):
+            zhp = plane(2 * near + lo + kind - 2 * lo * kind)[0]
+            for e in range(2):
+                for part in range(2):
+                    for y in range(4):
+                        start = pl.multiple_of(64 * y + 16 * zhp, 16)
+                        wy_ref[e, part, pl.ds(128 * kind + 64 * near + 16 * y, 16), :] = wh_ref[
+                            part, e, pl.ds(start, 16), :
+                        ]
+
     lane = lax.broadcasted_iota(jnp.int32, (HALF, 128), 1)
     is_edge = (lane == 0) | (lane == 64)
     turn = jnp.where(lane < 64, 1.0, -1.0).astype(F32)
 
     for h in range(2):
-        many = r1.at[pl.ds(0, 15), halves[h]]
+        many = r1.at[0, pl.ds(0, 15)]
         pltpu.make_async_copy(many, many, recv1.at[h]).wait()
         for e in range(2):
-            base = MIRROR + 4 * (1 - e)
 
             def fold(first, count):
-                top = r1[0:8, first : first + count]
-                bottom = r1[8:16, first : first + count]
+                top = r1[h, 0:8, first : first + count]
+                bottom = r1[h, 8:16, first : first + count]
                 return top + bottom if e == 0 else top - bottom
 
             edges = fold(0, 8)
-            for r in range(4):
-                i = 4 * h + r
-                direct = fold(8 + 32 * i, 32).reshape(HALF, 128)
-                edge = jnp.stack(
-                    [pltpu.roll(edges, 128 - 8 * k - i, 2) if k + i else edges for k in range(4)],
-                    axis=1,
-                ).reshape(HALF, 128)
-                mirror = jnp.where(is_edge, edge, direct)
-                plain = jnp.concatenate([direct, mirror], axis=1)
-                turned = jnp.concatenate(
-                    [pltpu.roll(direct, 64, 1) * turn, pltpu.roll(mirror, 64, 1) * turn], axis=1
-                )
-                hi, low = split(jnp.concatenate([plain, turned], axis=0))
-                out = mm(wh_ref[0, e], hi) + mm(wh_ref[1, e], hi) + mm(wh_ref[0, e], low)
-                zy[e, h, pl.ds(r, HALF, stride=4), :] = out[:, :128]
-                zy[e, h, pl.ds(base + r, HALF, stride=4), :] = out[:, 128:]
-                if e == 0:
-                    zy[e, h, pl.ds(base + 4 * HALF + r, 1), :] = out[0:1, 128:]
-
-            def start_for(dp, dl):
-                return (1 - dl) * (32 * dp) + dl * (base + 4 * (249 - e) - 32 * dp)
-
-            r2[e, h, lo, p] = zy[e, h, pl.ds(pl.multiple_of(start_for(p, lo), 8), 32), :]
+            for pair in range(4):
+                tiles = [[], []]
+                for r in (2 * pair, 2 * pair + 1):
+                    direct = fold(8 + 32 * r, 32).reshape(HALF, 128)
+                    edge = jnp.stack(
+                        [pltpu.roll(edges, 128 - 8 * k - r, 2) if k + r else edges for k in range(4)],
+                        axis=1,
+                    ).reshape(HALF, 128)
+                    tiles[0].append(direct)
+                    tiles[1].append(jnp.where(is_edge, edge, direct) * turn)
+                for kind in range(2):
+                    plain = jnp.concatenate(tiles[kind], axis=1)
+                    turned = jnp.concatenate([pltpu.roll(v, 64, 1) * turn for v in tiles[kind]], axis=1)
+                    hi, low = split(jnp.concatenate([plain, turned], axis=0))
+                    rows_of = pl.ds(128 * kind, 128)
+                    high, small = wy_ref[e, 0, rows_of, :], wy_ref[e, 1, rows_of, :]
+                    out = mm(high, hi) + mm(small, hi) + mm(high, low)
+                    for k in range(2):
+                        start = 1024 * kind + 2 * pair + k
+                        zy[e, h, pl.ds(start, 128, stride=8), :] = out[:, 128 * k : 128 * k + 128]
+
+            def start_for(kind, near, y, core):
+                return pl.multiple_of(8 * (128 * kind + 64 * near + 16 * y + 8 * core), 64)
+
+            r2[e, h, p] = zy[e, h, pl.ds(start_for(lo, 0, yc, c), 64), :]
             pieces = 2 if e and h else 1
-            size = 32 // pieces
+            size = 64 // pieces
             for piece in range(pieces):
 
-                def send_x(k, turn_y):
-                    part = lax.div(k + 1, 2)
-                    dz = lax.rem(2 * zh + lo + 4 + part * (1 - 2 * lax.rem(k, 2)), 8)
-                    dzh, dl = lax.div(dz, 2), lax.rem(dz, 2)
-                    dy = lax.rem(yc + turn_y // 2, 4)
-                    dc = lax.rem(c + turn_y % 2, 2)
-                    dp = dy * 8 + dzh * 2 + dc
-                    device = (dy, dzh, dc, dl, b + dl * (3 - 2 * b))
-                    skip = size * (piece + dl * (pieces - 1 - 2 * piece))
-                    start = start_for(dp, dl) + skip
+                def send_x(d, i):
+                    zhp, dl = plane(d)
+                    dy = lax.rem(yc + i // 2, 4)
+                    dc = lax.rem(c + i % 2, 2)
+                    start = start_for(dl, lax.div(d, 2), dy, dc) + size * piece
                     pltpu.make_async_remote_copy(
                         src_ref=zy.at[e, h, pl.ds(pl.multiple_of(start, 8), size), :],
-                        dst_ref=r2.at[e, h, lo, p, pl.ds(pl.multiple_of(skip, 8), size), :],
+                        dst_ref=r2.at[e, h, p, pl.ds(size * piece, size), :],
                         send_sem=send2.at[2 * h + e + piece],
                         recv_sem=recv2.at[2 * h + e + piece],
-                        device_id=device,
+                        device_id=(dy, zhp, dc, dl, b + dl * (3 - 2 * b)),
                         device_id_type=MESH,
                     ).start()
 
                 def send_plane(k, carry):
                     for i in range(8):
-                        send_x(k, i)
+                        send_x(3 - k, i)
                     return carry
 
-                lax.fori_loop(0, 7, send_plane, 0)
+                lax.fori_loop(0, 3, send_plane, 0)
                 for i in range(1, 8):
-                    send_x(7, i)
+                    send_x(jnp.int32(0), i)
 
     flip = lo
     row = lax.broadcasted_iota(jnp.int32, (128, 128), 0)
@@ -259,9 +270,7 @@
     within = jnp.where(upper, row - 64, row)
     negated = jnp.where(within == 0, 0, 64 - within)
     target = jnp.where(flip == 1, negated, within) + jnp.where(upper, 64, 0)
-    sign = jnp.where((flip == 1) & upper, -1.0, 1.0)
-    select = jnp.where(col == target, sign, 0.0).astype(BF16)
-    low_rows = lax.broadcasted_iota(jnp.int32, (32, 8, 128), 1) < 4
+    select = jnp.where(col == target, 1.0, 0.0).astype(BF16)
 
     def rows(v):
         return jnp.sum(v.reshape(8, 8, N), axis=0)
@@ -269,23 +278,18 @@
     for e in range(2):
 
         def arrived(block, size):
-            many = zy.at[0, 0, pl.ds(0, 63 * size), :]
+            many = zy.at[0, 0, pl.ds(0, 31 * size), :]
             pltpu.make_async_copy(many, many, recv2.at[block]).wait()
 
-        arrived(e, 32)
+        arrived(e, 64)
         if e == 0:
-            arrived(2, 32)
+            arrived(2, 64)
 
         def x_step(t, carry):
-            tile = t + flip * (3 - 2 * t)
-
             def turned(a):
-                top = r2[e, 0, a, :, pl.ds(pl.multiple_of(8 * tile, 8), 8), :]
-                bottom = r2[e, 1, a, :, pl.ds(pl.multiple_of(8 * tile, 8), 8), :]
-                slot0 = jnp.where(low_rows, top, pltpu.roll(bottom, 4, 1))
-                slot1 = jnp.where(low_rows, pltpu.roll(top, 4, 1), bottom)
                 his, lows = [], []
-                for v in (jnp.where(flip == 1, slot1, slot0), jnp.where(flip == 1, slot0, slot1)):
+                for j in range(2):
+                    v = r2[e, a, :, pl.ds(pl.multiple_of(8 * (2 * t + j), 8), 8), :]
                     hi, low = split(v.reshape(HALF, 128))
                     his.append(lax.dot_general(select, hi, NT, preferred_element_type=F32).astype(BF16))
                     lows.append(lax.dot_general(select, low, NT, preferred_element_type=F32).astype(BF16))
@@ -330,7 +334,7 @@
             lax.fori_loop(0, 4, x_step, 0)
         else:
             for piece in range(2):
-                arrived(3 + piece, 16)
+                arrived(3 + piece, 32)
                 x_step(2 * piece, 0)
                 x_step(2 * piece + 1, 0)
 
@@ -387,18 +391,14 @@
     virial_ref[...] = jnp.sum(jnp.where(lane8 == sub8 - 1, full, 0.0), axis=0, keepdims=True)[:, :6]
 
     for h in range(2):
-        many = r1.at[pl.ds(0, 15), halves[h]]
+        many = r1.at[0, pl.ds(0, 15)]
         pltpu.make_async_copy(many, many, send1.at[h]).wait()
-    for block, size in enumerate((32, 32, 32, 16, 16)):
-        sent = zy.at[0, 0, pl.ds(0, 63 * size), :]
+    for block, size in enumerate((64, 64, 64, 32, 32)):
+        sent = zy.at[0, 0, pl.ds(0, 31 * size), :]
         pltpu.make_async_copy(sent, sent, send2.at[block]).wait()
     for stage in range(2):
         many = first.at[pl.ds(0, 15)]
         pltpu.make_async_copy(many, many, send3.at[stage]).wait()
-
-
-MIRROR = 1024
-ROWS = 2064
 
 
 def body(charges_old, spline_moduli):
@@ -419,10 +419,11 @@
             pltpu.VMEM((2, 8, 2, 32, N), F32),
             pltpu.VMEM((2, N, 640), BF16),
             pltpu.VMEM((2, 2, HALF, N), BF16),
+            pltpu.VMEM((2, 2, HALF, N), BF16),
             pltpu.VMEM((4, 4, 264, 128), F32),
-            pltpu.VMEM((16, 264, 128), F32),
-            pltpu.VMEM((2, 2, ROWS, 128), F32),
-            pltpu.VMEM((2, 2, 2, 32, 32, 128), F32),
+            pltpu.VMEM((2, 16, 264, 128), F32),
+            pltpu.VMEM((2, 2, 2048, 128), F32),
+            pltpu.VMEM((2, 2, 32, 64, 128), F32),
             pltpu.VMEM((7, 8, N), F32),
             pltpu.VMEM((64, N), F32),
             pltpu.VMEM((64, N), F32),
@@ -439,7 +440,7 @@
             dma((2,)),
         ],
         compiler_params=pltpu.CompilerParams(
-            collective_id=0, has_side_effects=True, vmem_limit_bytes=24 * 2**20
+            collective_id=0, has_side_effects=True, vmem_limit_bytes=32 * 2**20
         ),
         name="ewald",
     )(

time: 147 us -> 159 us (1.082)
  Pallas kernels: 142 us -> 154 us
    pallas_call x1, Pallas kernels: 142 us -> 154 us  [body(): pl.pallas_call(ewald_kernel, out_shape=(jax.ShapeDtypeStruct((2, 8, 2, 64...]
where the time goes in v3:
time: 159 us
  Pallas kernels  154 us (97%)
  local copies, waits for them, and re-layouts  2.53 us (2%)
  between operations  2.33 us (1%)
    pallas_call x1, Pallas kernels, body(): pl.pallas_call(ewald_kernel, out_shape=(jax.ShapeDtypeStruct((2, 8, 2, 64...  154 us

profile of v3, /device:TPU:1, one launch (start us, length us, event | category | flops | bytes accessed | tf_op | source)
XLA Modules:
  0.0 158.9 jit_solution(11745562013867530037)
XLA Ops:
  0.6 154.0 %ewald.1 = (f32[2,8,2,64,512]{4,3,2,1,0:T(8,128)S(1)}, f32[1,1]{1,0:T(1,128)}, f32[1,6]{1,0:T(1,128)S(1)}) custom-call(f32[3,512]{1,0:T(4,128)} %mod_hbm.1, f32[2,8,2,32,512]{4,3,2,1,0:T(8,128)} %bitcast.6, bf16[2,512,640]{2,1,0:T(8,128)(2,1)} %constant.4.clone.wz_hbm, bf16[2,2,256,512]{3,2,1,0:T(8,128)(2,1)} %constant.5.clone.wh_hbm), custom_call_target="tpu_custom_call" | custom-call | tf_op jit(solution)/shard_map/ewald/pallas_call | solution.py:407
  154.7 2.0 %copy.10 = f32[2,16,64,512]{3,2,1,0:T(8,128)} copy(f32[2,16,64,512]{3,2,1,0:T(8,128)S(1)} %bitcast.4) | data formatting | bytes 8388608
  157.2 0.5 copy.12

commit v4 on v2

--- a/solution.py
+++ b/solution.py
@@ -220,7 +220,7 @@
                 return (1 - dl) * (32 * dp) + dl * (base + 4 * (249 - e) - 32 * dp)
 
             r2[e, h, lo, p] = zy[e, h, pl.ds(pl.multiple_of(start_for(p, lo), 8), 32), :]
-            pieces = 2 if e and h else 1
+            pieces = 4 if e and h else 1
             size = 32 // pieces
             for piece in range(pieces):
 
@@ -329,16 +329,17 @@
         if e == 0:
             lax.fori_loop(0, 4, x_step, 0)
         else:
-            for piece in range(2):
-                arrived(3 + piece, 16)
-                x_step(2 * piece, 0)
-                x_step(2 * piece + 1, 0)
+            for piece in range(4):
+                arrived(3 + piece, 8)
+                x_step(piece, 0)
 
     def lanes(v):
         v = jnp.sum(v, axis=0, keepdims=True)
         return v[:, 0:128] + v[:, 128:256] + v[:, 256:384] + v[:, 384:512]
 
-    parts[...] = jnp.concatenate(
+    sub8 = lax.broadcasted_iota(jnp.int32, (8, 128), 0)
+    lane8 = lax.broadcasted_iota(jnp.int32, (8, 128), 1)
+    column = jnp.concatenate(
         [
             lanes(acc[0]),
             lanes(acc[1] * (mx * mx)),
@@ -351,6 +352,8 @@
         ],
         axis=0,
     )
+    column = jnp.sum(column, axis=1, keepdims=True)
+    parts[...] = jnp.sum(jnp.where(lane8 == sub8, column, 0.0), axis=0, keepdims=True)
 
     def spread(stage, source, slots, me):
         slots[me] = source[...]
@@ -378,18 +381,15 @@
         return jnp.sum(slots[...], axis=0)
 
     middle[...] = spread(0, parts, first, me16)
-    totals = jnp.sum(spread(1, middle, second, outer), axis=1, keepdims=True)
-    energy = 0.5 * totals[0:1]
-    energy_ref[...] = energy
-    sub8 = lax.broadcasted_iota(jnp.int32, (8, 128), 0)
-    lane8 = lax.broadcasted_iota(jnp.int32, (8, 128), 1)
-    full = jnp.where((sub8 >= 1) & (sub8 <= 3), energy, 0.0) - totals
-    virial_ref[...] = jnp.sum(jnp.where(lane8 == sub8 - 1, full, 0.0), axis=0, keepdims=True)[:, :6]
+    totals = jnp.broadcast_to(spread(1, middle, second, outer), (8, 128))
+    energy = 0.5 * totals[:, 0:1]
+    energy_ref[...] = energy[0:1]
+    virial_ref[...] = (jnp.where(lane8 < 3, energy, 0.0) - pltpu.roll(totals, 127, 1))[0:1, :6]
 
     for h in range(2):
         many = r1.at[pl.ds(0, 15), halves[h]]
         pltpu.make_async_copy(many, many, send1.at[h]).wait()
-    for block, size in enumerate((32, 32, 32, 16, 16)):
+    for block, size in enumerate((32, 32, 32, 8, 8, 8, 8)):
         sent = zy.at[0, 0, pl.ds(0, 63 * size), :]
         pltpu.make_async_copy(sent, sent, send2.at[block]).wait()
     for stage in range(2):
@@ -426,15 +426,15 @@
             pltpu.VMEM((7, 8, N), F32),
             pltpu.VMEM((64, N), F32),
             pltpu.VMEM((64, N), F32),
-            pltpu.VMEM((8, 128), F32),
-            pltpu.VMEM((16, 8, 128), F32),
-            pltpu.VMEM((8, 128), F32),
-            pltpu.VMEM((16, 8, 128), F32),
+            pltpu.VMEM((1, 128), F32),
+            pltpu.VMEM((16, 1, 128), F32),
+            pltpu.VMEM((1, 128), F32),
+            pltpu.VMEM((16, 1, 128), F32),
             dma((5,)),
             dma((2,)),
             dma((2,)),
-            dma((5,)),
-            dma((5,)),
+            dma((7,)),
+            dma((7,)),
             dma((2,)),
             dma((2,)),
         ],

time: 147 us -> 147 us (level)
  no operation moved by 1% of the time
where the time goes in v4:
time: 147 us
  Pallas kernels  142 us (97%)
  local copies, waits for them, and re-layouts  2.53 us (2%)
  between operations  2.33 us (2%)
    pallas_call x1, Pallas kernels, body(): pl.pallas_call(ewald_kernel, out_shape=(jax.ShapeDtypeStruct((2, 8, 2, 64...  142 us

profile of v4, /device:TPU:1, one launch (start us, length us, event | category | flops | bytes accessed | tf_op | source)
XLA Modules:
  0.0 146.5 jit_solution(3499550738808674543)
XLA Ops:
  0.6 141.6 %ewald.1 = (f32[2,8,2,64,512]{4,3,2,1,0:T(8,128)S(1)}, f32[1,1]{1,0:T(1,128)}, f32[1,6]{1,0:T(1,128)S(1)}) custom-call(f32[3,512]{1,0:T(4,128)} %mod_hbm.1, f32[2,8,2,32,512]{4,3,2,1,0:T(8,128)} %bitcast.6, bf16[2,512,640]{2,1,0:T(8,128)(2,1)} %constant.4.clone.wz_hbm, bf16[2,2,256,512]{3,2,1,0:T(8,128)(2,1)} %constant.5.clone.wh_hbm), custom_call_target="tpu_custom_call" | custom-call | tf_op jit(solution)/shard_map/ewald/pallas_call | solution.py:407
  142.3 2.0 %copy.10 = f32[2,16,64,512]{3,2,1,0:T(8,128)} copy(f32[2,16,64,512]{3,2,1,0:T(8,128)S(1)} %bitcast.4) | data formatting | bytes 8388608
  144.9 0.5 copy.12

commit v5 on v4

--- a/solution.py
+++ b/solution.py
@@ -75,9 +75,9 @@
     mod_smem, mod_ref, x_ref, wz_ref, wh_ref, zs, r1, zy, r2, acc, xz2, modxz, parts, first, middle, second,
     load, send1, recv1, send2, recv2, send3, recv3,
 ):
-    tables = (
-        (x_hbm, x_ref), (wz_hbm, wz_ref), (wh_hbm, wh_ref), (mod_hbm, mod_ref), (mod_hbm, mod_smem)
-    )
+    tables = [(wz_hbm, wz_ref)]
+    tables += [(x_hbm.at[g // 2, :, g % 2], x_ref.at[g // 2, :, g % 2]) for g in range(4)]
+    tables += [(wh_hbm, wh_ref), (mod_hbm, mod_ref), (mod_hbm, mod_smem)]
     loads = [pltpu.make_async_copy(a, b, load.at[i]) for i, (a, b) in enumerate(tables)]
     for copy in loads:
         copy.start()
@@ -121,7 +121,7 @@
     narrow = lax.rem(lax.broadcasted_iota(jnp.int32, (32, 128), 1), 64) < 8
 
     def z_step(g, carry):
-        rows = x_ref[lax.div(g, 2), :, lax.rem(g, 2)].reshape(256, N)
+        rows = x_ref[g // 2, :, g % 2].reshape(256, N)
         hi, low = split(rows)
         out = mm(hi, wz_ref[0]) + mm(low, wz_ref[0]) + mm(hi, wz_ref[1])
         for k in range(4):
@@ -142,8 +142,9 @@
         return carry
 
     loads[0].wait()
-    loads[1].wait()
-    lax.fori_loop(0, 4, z_step, 0)
+    for g in range(4):
+        loads[1 + g].wait()
+        z_step(g, 0)
     pl.semaphore_wait(barrier, 78)
 
     halves = (pl.ds(0, 136), pl.ds(136, 128))
@@ -168,8 +169,8 @@
         lax.fori_loop(9, 16, send_y, 0, unroll=7)
     r1[me16] = zs[2 * c + lo, b]
 
-    loads[3].wait()
-    loads[4].wait()
+    loads[6].wait()
+    loads[7].wait()
     mx = signed_wave(lax.broadcasted_iota(jnp.int32, (1, N), 1))
     mz = signed_wave(64 * (4 * lo + xc) + lax.broadcasted_iota(jnp.int32, (64, 1), 0))
     acc[...] = jnp.zeros_like(acc)
@@ -179,7 +180,7 @@
     modz = jnp.concatenate([modz] * 4, axis=1)
     modxz[...] = mod_ref[0:1, :] * modz * (1.0 / (math.pi * (cell_nm * N) ** 3))
 
-    loads[2].wait()
+    loads[5].wait()
 
     lane = lax.broadcasted_iota(jnp.int32, (HALF, 128), 1)
     is_edge = (lane == 0) | (lane == 64)
@@ -430,7 +431,7 @@
             pltpu.VMEM((16, 1, 128), F32),
             pltpu.VMEM((1, 128), F32),
             pltpu.VMEM((16, 1, 128), F32),
-            dma((5,)),
+            dma((8,)),
             dma((2,)),
             dma((2,)),
             dma((7,)),

time: 147 us -> 147 us (level)
  no operation moved by 1% of the time
where the time goes in v5:
time: 147 us
  Pallas kernels  142 us (97%)
  local copies, waits for them, and re-layouts  2.53 us (2%)
  between operations  2.33 us (2%)
    pallas_call x1, Pallas kernels, body(): pl.pallas_call(ewald_kernel, out_shape=(jax.ShapeDtypeStruct((2, 8, 2, 64...  142 us

profile of v5, /device:TPU:1, one launch (start us, length us, event | category | flops | bytes accessed | tf_op | source)
XLA Modules:
  0.0 146.5 jit_solution(3920675145534938109)
XLA Ops:
  0.6 141.7 %ewald.1 = (f32[2,8,2,64,512]{4,3,2,1,0:T(8,128)S(1)}, f32[1,1]{1,0:T(1,128)}, f32[1,6]{1,0:T(1,128)S(1)}) custom-call(f32[3,512]{1,0:T(4,128)} %mod_hbm.1, f32[2,8,2,32,512]{4,3,2,1,0:T(8,128)} %bitcast.6, bf16[2,512,640]{2,1,0:T(8,128)(2,1)} %constant.4.clone.wz_hbm, bf16[2,2,256,512]{3,2,1,0:T(8,128)(2,1)} %constant.5.clone.wh_hbm), custom_call_target="tpu_custom_call" | custom-call | tf_op jit(solution)/shard_map/ewald/pallas_call | solution.py:408
  142.3 2.0 %copy.10 = f32[2,16,64,512]{3,2,1,0:T(8,128)} copy(f32[2,16,64,512]{3,2,1,0:T(8,128)S(1)} %bitcast.4) | data formatting | bytes 8388608
  144.9 0.5 copy.12
